TPU v7x, 1024 devices: a whole 8x8x8 slice. The times are simulated.
1024 devices in a mesh: dp: 16 (over x, core), seq: 8 (over z), tensor: 8 (over y).
Axes of the slice: x: 8, y: 8, z: 8, core: 2. Of those that a mesh axis runs over, the one named last changes fastest.
Arguments:
- vit_out: bfloat16 [32768, 3200], P(('dp', 'seq')), may hold values from -6 to 6
- ln_gain: float32 [3200], replicated, may hold values from 0.1 to 1.9
- ln_bias: float32 [3200], replicated, may hold values from -3 to 3
- proj_weight: bfloat16 [3200, 8, 1024], P(None, None, 'tensor'), may hold values from -0.109375 to 0.109375
- proj_bias: float32 [8, 1024], P(None, 'tensor'), may hold values from -3 to 3
- text_embed: bfloat16 [65536, 8192], P('dp', ('seq', 'tensor')), may hold values from -6 to 6
- norm_gain: float32 [8192], P(('seq', 'tensor')), may hold values from 0.1 to 1.9
- tile_dest: int32 [256, 1], replicated, may hold values from 0 to 15; in each aligned block of 16 rows (0 to 15, 16 to 31, ...) at most 2 rows name the same one
- tile_place: int32 [16, 32], replicated, may hold values from 0 to 31, each once within a row
Outputs:
- normed: bfloat16 [65536, 8192], P('dp', ('seq', 'tensor'))
Inputs may be any that keep to these rules, and one draw needn't show every extreme that they name: `tile_dest`: in each aligned block of 16 rows (one encoder group's tiles) no replica is named more than 2 times, a bound that some block reaches. `tile_place`: each row is a permutation of 0 to 31.
All inputs are finite; a program needn't handle non-finite values.
Results may differ from a plain program's by a relative error of at most 0.0048.
Values may be sent and summed in bfloat16 or wider, within the bound.
A program may use at most 64 MiB of HBM per device.

v0:
```python
import jax
import jax.numpy as jnp
from jax import lax
from jax.sharding import PartitionSpec as P

D = 8192
TILE = 128


def from_everyone(array, axis):
    copies = jnp.broadcast_to(array, (lax.axis_size(axis), *array.shape))
    return lax.all_to_all(copies, axis, split_axis=0, concat_axis=0, tiled=True)


def of_everyone(array, axis):
    everything = from_everyone(array, axis)
    return jnp.sum(everything, axis=0)


def layer_norm(rows, ln_gain, ln_bias):
    values = rows.astype(jnp.float32)
    center = values - jnp.mean(values, axis=-1, keepdims=True)
    spread = jnp.mean(center * center, axis=-1, keepdims=True)
    return (center * lax.rsqrt(spread + 1e-06) * ln_gain + ln_bias).astype(jnp.bfloat16)


def arrival_ranks(destination, replicas):
    onehot = (destination[:, None] == jnp.arange(replicas, dtype=jnp.int32)[None, :]).astype(
        jnp.int32
    )
    before = jnp.cumsum(onehot, axis=0) - onehot
    return jnp.sum(before * onehot, axis=1)


def row_squares(rows):
    values = rows.astype(jnp.float32)
    return jnp.sum(values * values, axis=-1)


def local(
    vit_out, ln_gain, ln_bias, proj_weight, proj_bias, text_embed, norm_gain, tile_dest, tile_place
):
    replicas = lax.axis_size("dp")
    owners = lax.axis_size("seq")
    my_replica = lax.axis_index("dp")
    local_rows = vit_out.shape[0]
    width_in = vit_out.shape[1]
    column_block = proj_weight.shape[2]
    positions = tile_place.shape[1]
    seq_rows = text_embed.shape[0]
    group_tiles = owners * local_rows // TILE
    total_tiles = tile_dest.shape[0]
    normed_in = layer_norm(vit_out, ln_gain, ln_bias)
    weights_flat = proj_weight.reshape(width_in, owners * column_block)
    hidden = jnp.dot(
        normed_in, weights_flat, preferred_element_type=jnp.float32
    ) + proj_bias.reshape(-1)
    projected = hidden.astype(jnp.bfloat16)
    regrouped = lax.all_to_all(
        projected.reshape(local_rows, owners, column_block),
        "seq",
        split_axis=1,
        concat_axis=0,
        tiled=True,
    )
    group_rows = regrouped.reshape(owners * local_rows, column_block)
    destination = tile_dest[:, 0]
    ranks = arrival_ranks(destination, replicas)
    place_row = lax.dynamic_index_in_dim(tile_place, my_replica, 0, keepdims=False)
    slot_of_tile = jnp.where(
        destination == my_replica, jnp.take(place_row, jnp.minimum(ranks, positions - 1)), -1
    )
    matches = slot_of_tile[None, :] == jnp.arange(positions, dtype=jnp.int32)[:, None]
    source_tile = (
        jnp.sum(
            matches.astype(jnp.int32) * (jnp.arange(total_tiles, dtype=jnp.int32) + 1)[None, :],
            axis=1,
        )
        - 1
    )
    text_tiles = text_embed.reshape(positions, TILE, column_block)
    capacity = max(2, 2 * group_tiles // replicas)
    local_dest = lax.dynamic_slice_in_dim(destination, my_replica * group_tiles, group_tiles)
    local_rank = arrival_ranks(local_dest, replicas)
    slot_index = local_dest * capacity + local_rank
    filling = slot_index[None, :] == jnp.arange(replicas * capacity, dtype=jnp.int32)[:, None]
    slot_source = (
        jnp.sum(
            filling.astype(jnp.int32) * (jnp.arange(group_tiles, dtype=jnp.int32) + 1)[None, :],
            axis=1,
        )
        - 1
    )
    tiles = group_rows.reshape(group_tiles, TILE, column_block)
    outgoing = jnp.where(
        (slot_source >= 0)[:, None, None],
        tiles[jnp.clip(slot_source, 0, group_tiles - 1)],
        jnp.zeros((), jnp.bfloat16),
    )
    outgoing = outgoing.reshape(replicas, capacity, TILE, column_block)
    incoming = lax.all_to_all(outgoing, "dp", split_axis=0, concat_axis=0, tiled=True).reshape(
        replicas * capacity, TILE, column_block
    )
    group_ranks = jax.vmap(lambda block: arrival_ranks(block, replicas))(
        destination.reshape(replicas, group_tiles)
    ).reshape(-1)
    safe_tile = jnp.clip(source_tile, 0, total_tiles - 1)
    arrival_index = safe_tile // group_tiles * capacity + jnp.take(group_ranks, safe_tile)
    picked = incoming[jnp.clip(arrival_index, 0, replicas * capacity - 1)]
    assembled = jnp.where((source_tile >= 0)[:, None, None], picked, text_tiles).reshape(
        seq_rows, column_block
    )
    squares = row_squares(assembled)
    totals = of_everyone(squares, ("seq", "tensor"))
    scale = lax.rsqrt(totals / D + 1e-05)
    return (assembled.astype(jnp.float32) * scale[:, None] * norm_gain).astype(jnp.bfloat16)


def solution(mesh):
    placed = (
        P(("dp", "seq"), None),
        P(),
        P(),
        P(None, None, "tensor"),
        P(None, "tensor"),
        P("dp", ("seq", "tensor")),
        P(("seq", "tensor")),
        P(),
        P(),
    )
    return jax.shard_map(
        local, mesh=mesh, in_specs=placed, out_specs=P("dp", ("seq", "tensor")), check_vma=False
    )
```

profile of v0, /device:TPU:1, one launch (start us, length us, event | category | flops | bytes accessed | tf_op | source)
XLA Modules:
  0.0 127.2 jit_solution(1772689207826924300)
XLA Ops:
  0.0 1.9 %convert_reduce_fusion = f32[256]{0:T(256)S(1)} fusion(bf16[256,3200]{1,0:T(8,128)(2,1)} %param.9), kind=kLoop, calls=%fused_computation.7 | loop fusion | flops 1638144 | bytes 1639424 | tf_op jit(solution)/shard_map/reduce_sum | solution.py:22
  1.9 2.0 %fusion.5 = f32[256]{0:T(256)S(1)} fusion(bf16[256,3200]{1,0:T(8,128)(2,1)} %param.9, f32[256]{0:T(256)S(1)} %broadcast_multiply_fusion), kind=kLoop, calls=%fused_computation.10 | loop fusion | flops 3276544 | bytes 1640448 | tf_op jit(solution)/shard_map/reduce_sum | solution.py:23
  4.0 4.9 %fusion.27 = bf16[32,8,8,128]{3,2,1,0:T(8,128)(2,1)S(1)} fusion(bf16[400,8,8,128]{3,2,1,0:T(8,128)(2,1)} %bitcast.128, bf16[256,3200]{1,0:T(8,128)(2,1)S(1)} %copy-done.1, f32[3200]{0:T(1024)S(1)} %copy-done.5, f32[3200]{0:T(1024)S(1)} %copy-done.6, f32[256]{0:T(256)S(1)} %add_rsqrt_fusion.1, f32[256]{0:T(256)S(1)} %broadcast_multiply_fusion, ...), kind=kOutput, calls=%fused_computation.25 | convolution fusion | flops 1683161088 | bytes 8748032 | tf_op jit(solution)/shard_map/dot_general | solution.py:55
  8.8 0.9 copy.46
  9.7 17.2 %all-to-all-start = ((bf16[256,8,128]{2,0,1:T(8,128)(2,1)}), bf16[256,8,128]{2,0,1:T(8,128)(2,1)S(1)}, u32[]{:S(2)}, u32[]{:S(2)}) async-start(bf16[256,8,128]{2,0,1:T(8,128)(2,1)} %bitcast.119), calls=%async_computation | async-start | bytes 1048576 | tf_op jit(solution)/shard_map/all_to_all | solution.py:59
  27.5 0.6 reduce-window.6
  28.3 0.6 broadcast.696
  28.9 0.7 reduce.56
  29.9 0.7 fusion.45
  31.2 13.7 %all-to-all-done = bf16[256,8,128]{2,0,1:T(8,128)(2,1)S(1)} async-done(((bf16[256,8,128]{2,0,1:T(8,128)(2,1)}), bf16[256,8,128]{2,0,1:T(8,128)(2,1)S(1)}, u32[]{:S(2)}, u32[]{:S(2)}) %all-to-all-start) | async-done | bytes 524320 | tf_op jit(solution)/shard_map/all_to_all | solution.py:59
  44.9 0.7 gather_fusion
  45.7 1.1 broadcast_select_fusion
  46.8 7.3 %all-to-all-start.1 = ((bf16[16,2,128,128]{3,2,1,0:T(8,128)(2,1)}), bf16[16,2,128,128]{3,2,1,0:T(8,128)(2,1)S(1)}, u32[]{:S(2)}, u32[]{:S(2)}) async-start(bf16[16,2,128,128]{3,2,1,0:T(8,128)(2,1)} %broadcast_select_fusion), calls=%async_computation.1 | async-start | bytes 2097152 | tf_op jit(solution)/shard_map/all_to_all | solution.py:101
  54.2 0.7 fusion.44
  54.9 4.5 %compare_select_fusion.1 = (s32[256,1]{0,1:T(1,128)S(1)}, s32[256,1]{0,1:T(1,128)S(1)}) fusion(s32[]{:T(128)} %bitcast.29, s32[]{:T(128)} %bitcast.30, s32[]{:T(128)} %bitcast.31, s32[]{:T(128)} %bitcast.32, s32[]{:T(128)} %bitcast.33, s32[]{:T(128)} %bitcast.35, s32[]{:T(128)} %bitcast.34, s32[256,1]{0,1:T(1,128)S(1)} %bitcast.126), kind=kLoop, calls=%fused_computation.81 | loop fusion | flops 3840 | bytes 3100 | tf_op jit(solution)/shard_map/jit(_take)/gather | solution.py:71
  59.5 15.6 %compare_select_fusion.10 = s32[256]{0:T(256)S(1)} fusion(s32[256]{0:T(256)S(1)} %bitcast.125, pred[256]{0:T(512)(128)(4,1)S(1)} %get-tuple-element.29, pred[256]{0:T(512)(128)(4,1)S(1)} %get-tuple-element.28, pred[256]{0:T(512)(128)(4,1)S(1)} %get-tuple-element.27, pred[256]{0:T(512)(128)(4,1)S(1)} %get-tuple-element.26, ...), kind=kLoop, calls=%fused_computation.93 | loop fusion | flops 8960 | bytes 10600 | tf_op jit(solution)/shard_map/jit(_where)/select_n | solution.py:70
  75.2 0.7 gather_fusion.1
  76.1 6.0 %all-to-all-done.1 = bf16[16,2,128,128]{3,2,1,0:T(8,128)(2,1)S(1)} async-done(((bf16[16,2,128,128]{3,2,1,0:T(8,128)(2,1)}), bf16[16,2,128,128]{3,2,1,0:T(8,128)(2,1)S(1)}, u32[]{:S(2)}, u32[]{:S(2)}) %all-to-all-start.1) | async-done | bytes 1048608 | tf_op jit(solution)/shard_map/all_to_all | solution.py:101
  82.0 0.7 gather_fusion.2
  82.8 1.4 %fusion.9 = f32[4096]{0:T(1024)S(1)} fusion(bf16[4096,128]{1,0:T(8,128)(2,1)S(1)} %copy-done.2, bf16[32,128,128]{2,1,0:T(8,128)(2,1)S(1)} %gather_fusion.2, pred[4096]{0:T(1024)(128)(4,1)S(1)} %broadcast_bitcast_fusion), kind=kLoop, calls=%fused_computation.16 | loop fusion | flops 2093056 | bytes 2117632 | tf_op jit(solution)/shard_map/reduce_sum | solution.py:37
  84.2 1.0 broadcast_in_dim.71
  85.2 37.2 %all_to_all.26 = f32[64,1,4096]{2,1,0:T(1,128)S(1)} all-to-all(f32[64,1,4096]{2,1,0:T(1,128)S(1)} %broadcast_in_dim.71), channel_id=1, replica_groups=mesh['dp'=16,'seq'=8,'tensor'=8] {'seq','tensor'}, dimensions={0} | all-to-all | bytes 2097152 | tf_op jit(solution)/shard_map/all_to_all | solution.py:12
  122.5 0.9 reduce_sum.89
  123.4 3.7 %fusion.11 = bf16[4096,128]{1,0:T(8,128)(2,1)} fusion(f32[128]{0:T(128)S(1)} %copy-done.4, f32[4096]{0:T(1024)S(1)} %add_rsqrt_fusion, bf16[4096,128]{1,0:T(8,128)(2,1)S(1)} %copy-done.2, bf16[32,128,128]{2,1,0:T(8,128)(2,1)S(1)} %gather_fusion.2, pred[4096]{0:T(1024)(128)(4,1)S(1)} %broadcast_bitcast_fusion), kind=kLoop, calls=%fused_computation.18 | loop fusion | flops 2621440 | bytes 3166720 | tf_op jit(solution)/shard_map/convert_element_type | solution.py:116
  (50 shorter events, 2.2 us)
Async XLA Ops:
  0.0 29.9 %copy-start = (s32[16,32]{1,0:T(8,128)S(1)}, s32[16,32]{1,0:T(8,128)}, u32[]{:S(2)}) copy-start(s32[16,32]{1,0:T(8,128)} %param.17) | copy-start | bytes 6148
  0.0 3.9 %copy-start.1 = (bf16[256,3200]{1,0:T(8,128)(2,1)S(1)}, bf16[256,3200]{1,0:T(8,128)(2,1)}, u32[]{:S(2)}) copy-start(bf16[256,3200]{1,0:T(8,128)(2,1)} %param.9) | copy-start | bytes 4915204
  0.0 3.9 %copy-start.7 = (f32[8,128]{1,0:T(8,128)S(1)}, f32[8,128]{1,0:T(8,128)}, u32[]{:S(2)}) copy-start(f32[8,128]{1,0:T(8,128)} %param.13) | copy-start | bytes 12292
  0.0 3.9 %copy-start.5 = (f32[3200]{0:T(1024)S(1)}, f32[3200]{0:T(1024)}, u32[]{:S(2)}) copy-start(f32[3200]{0:T(1024)} %param.11) | copy-start | bytes 38404
  0.0 3.9 %copy-start.6 = (f32[3200]{0:T(1024)S(1)}, f32[3200]{0:T(1024)}, u32[]{:S(2)}) copy-start(f32[3200]{0:T(1024)} %param.10) | copy-start | bytes 38404
  3.9 23.0 %copy-start.3 = (s32[256,1]{0,1:T(1,128)S(1)}, s32[256,1]{0,1:T(1,128)}, u32[]{:S(2)}) copy-start(s32[256,1]{0,1:T(1,128)} %param.16) | copy-start | bytes 3076
  9.7 35.2 %all-to-all-start = ((bf16[256,8,128]{2,0,1:T(8,128)(2,1)}), bf16[256,8,128]{2,0,1:T(8,128)(2,1)S(1)}, u32[]{:S(2)}, u32[]{:S(2)}) async-start(bf16[256,8,128]{2,0,1:T(8,128)(2,1)} %bitcast.119), calls=%async_computation | async-start | bytes 1048576 | tf_op jit(solution)/shard_map/all_to_all | solution.py:59
  45.6 37.1 %copy-start.2 = (bf16[4096,128]{1,0:T(8,128)(2,1)S(1)}, bf16[4096,128]{1,0:T(8,128)(2,1)}, u32[]{:S(2)}) copy-start(bf16[4096,128]{1,0:T(8,128)(2,1)} %param.14) | copy-start | bytes 3145732
  46.8 35.3 %all-to-all-start.1 = ((bf16[16,2,128,128]{3,2,1,0:T(8,128)(2,1)}), bf16[16,2,128,128]{3,2,1,0:T(8,128)(2,1)S(1)}, u32[]{:S(2)}, u32[]{:S(2)}) async-start(bf16[16,2,128,128]{3,2,1,0:T(8,128)(2,1)} %broadcast_select_fusion), calls=%async_computation.1 | async-start | bytes 2097152 | tf_op jit(solution)/shard_map/all_to_all | solution.py:101
  82.8 40.6 %copy-start.4 = (f32[128]{0:T(128)S(1)}, f32[128]{0:T(128)}, u32[]{:S(2)}) copy-start(f32[128]{0:T(128)} %param.15) | copy-start | bytes 1540
where the time goes:
time: 128 us; the launch traced here: 127 us
  blocking collectives  37.2 us (29%)
  other arithmetic  33.7 us (26%)
  starting transfers between devices  24.5 us (19%)
  waiting for transfers between devices  19.7 us (15%)
  local copies, waits for them, and re-layouts  6.92 us (5%)
  matrix products  4.86 us (4%)
    all_to_all x1, blocking collectives, from_everyone(): return lax.all_to_all(copies, axis, split_axis=0, concat_axis=0, tiled=True)  37.2 us
    all_to_all x1, starting transfers between devices, local(): lax.all_to_all(projected.reshape(local_rows, owners, column_block), 'seq'...  17.2 us
    select_n x1, other arithmetic, local(): jnp.where(destination == my_replica, jnp.take(place_row, jnp.minimum(rank...  15.6 us
    all_to_all x1, waiting for transfers between devices, local(): lax.all_to_all(projected.reshape(local_rows, owners, column_block), 'seq'...  13.7 us
    all_to_all x1, starting transfers between devices, local(): lax.all_to_all(outgoing, 'dp', split_axis=0, concat_axis=0, tiled=True)  7.27 us
    all_to_all x1, waiting for transfers between devices, local(): lax.all_to_all(outgoing, 'dp', split_axis=0, concat_axis=0, tiled=True)  5.97 us
    dot_general x1, matrix products, local(): jnp.dot(normed_in, weights_flat, preferred_element_type=jnp.float32)  4.86 us
    gather x2, other arithmetic, local(): jnp.take(place_row, jnp.minimum(ranks, positions - 1))  4.58 us
  transfers between devices with their start and end apart: 2, of which 2 were waited for; matrix products, arithmetic and copies ran while one was open for 21% of the time, Pallas kernels for 0%

commit v1 on v0

v1 whole, which is shorter than its diff:
```python
import functools

import jax
import jax.numpy as jnp
from jax import lax
from jax.experimental import pallas as pl
from jax.experimental.pallas import tpu as pltpu
from jax.sharding import PartitionSpec as P

D = 8192
TILE = 128
CAP = 2
CHUNKS = 4
MESH = pl.DeviceIdType.MESH


def layer_norm(rows, ln_gain, ln_bias):
    values = rows.astype(jnp.float32)
    center = values - jnp.mean(values, axis=-1, keepdims=True)
    spread = jnp.mean(center * center, axis=-1, keepdims=True)
    return (center * lax.rsqrt(spread + 1e-06) * ln_gain + ln_bias).astype(jnp.bfloat16)


def spiral(n):
    order = [n // 2]
    for d in range(n // 2 - 1, 0, -1):
        order += [d, n - d]
    return order


def lane_sums(squares):
    ones = jnp.ones((8, squares.shape[1]), jnp.bfloat16)
    dims = (((1,), (1,)), ((), ()))
    high = squares.astype(jnp.bfloat16)
    low = (squares - high.astype(jnp.float32)).astype(jnp.bfloat16)
    return lax.dot_general(
        ones, high, dims, preferred_element_type=jnp.float32
    ) + lax.dot_general(ones, low, dims, preferred_element_type=jnp.float32)


def exchange_kernel(
    sizes,
    proj,
    text_hbm,
    gain,
    dest,
    place,
    out_hbm,
    text,
    out,
    scales,
    part,
    ybuf,
    zbuf,
    isums,
    tsums,
    xsend,
    xsums,
    table,
    kinv,
    starts,
    *rest,
):
    replicas, owners, tensors, positions = sizes
    rows = TILE // CHUNKS
    group_tiles = 2 * owners
    tiles, slots, inc = rest[:CHUNKS], rest[CHUNKS : 2 * CHUNKS], rest[2 * CHUNKS : 3 * CHUNKS]
    (zs, zr, xs, xr, ys, yr, zss, zsr, xss, xsr, tsem, osem) = rest[3 * CHUNKS :]
    me_dp, me_s, me_t = lax.axis_index("dp"), lax.axis_index("seq"), lax.axis_index("tensor")

    def peer(me, k, n):
        return lax.rem(me + k, n)

    barrier = pltpu.get_barrier_semaphore()
    axes = (("dp", me_dp, replicas), ("seq", me_s, owners), ("tensor", me_t, tensors))
    for name, me, n in axes:
        for k in spiral(n):
            pl.semaphore_signal(
                barrier, inc=1, device_id={name: peer(me, k, n)}, device_id_type=MESH
            )
    load_text = pltpu.make_async_copy(text_hbm, text, tsem)
    load_text.start()
    pl.semaphore_wait(barrier, replicas + owners + tensors - 3)

    zcopies = []
    for h in range(CHUNKS):
        for k in spiral(owners):
            to = peer(me_s, k, owners)
            zcopies.append(
                pltpu.make_async_remote_copy(
                    src_ref=proj.at[to, :, pl.ds(h * rows, rows), :],
                    dst_ref=tiles[h].at[pl.ds(2 * me_s, 2)],
                    send_sem=zs.at[h, k],
                    recv_sem=zr.at[h, k],
                    device_id={"seq": to},
                    device_id_type=MESH,
                )
            )
            zcopies[-1].start()
    for h in range(CHUNKS):
        tiles[h][pl.ds(2 * me_s, 2)] = proj[me_s, :, h * rows : (h + 1) * rows, :]

    load_text.wait()
    sub = lax.broadcasted_iota(jnp.int32, (8, TILE), 0)

    def sum_text(b, carry):
        values = text[pl.ds(8 * b, 8)].astype(jnp.float32).reshape(8 * TILE, TILE)
        sums = lane_sums(values * values)
        total = jnp.zeros((8, TILE), jnp.float32)
        for i in range(8):
            total = jnp.where(sub == i, sums[:, i * TILE : (i + 1) * TILE], total)
        part[pl.ds(pl.multiple_of(8 * b, 8), 8), :] = total
        return carry

    lax.fori_loop(0, positions // 8, sum_text, 0)
    squares = jnp.zeros((2 * TILE, TILE), jnp.float32)
    for s in range(owners):
        values = proj[s].astype(jnp.float32).reshape(2 * TILE, TILE)
        squares = squares + values * values
    sums = lane_sums(squares)
    part[positions : positions + 8, :] = jnp.where(sub == 0, sums[:, :TILE], sums[:, TILE:])

    ycopies = []
    for k in spiral(tensors):
        to = peer(me_t, k, tensors)
        ycopies.append(
            pltpu.make_async_remote_copy(
                src_ref=part,
                dst_ref=ybuf.at[me_t],
                send_sem=ys.at[k],
                recv_sem=yr.at[k],
                device_id={"tensor": to},
                device_id_type=MESH,
            )
        )
        ycopies[-1].start()

    for r in range(replicas):
        first = jnp.int32(group_tiles - 1)
        last = jnp.int32(0)
        for j in range(group_tiles):
            hit = dest[me_dp * group_tiles + j] == r
            last = jnp.where(hit, j, last)
            hit_back = dest[me_dp * group_tiles + group_tiles - 1 - j] == r
            first = jnp.where(hit_back, group_tiles - 1 - j, first)
        table[2 * r] = first
        table[2 * r + 1] = last

    def count(g, total):
        starts[g] = total
        for j in range(group_tiles):
            total = total + jnp.where(dest[g * group_tiles + j] == me_dp, 1, 0)
        return total

    starts[replicas] = lax.fori_loop(0, replicas, count, jnp.int32(0))

    def invert(p, carry):
        order = jnp.int32(0)
        for k in range(positions):
            order = jnp.where(place[me_dp, k] == p, k, order)
        slot = jnp.int32(-1)
        for g in range(replicas):
            here = (order >= starts[g]) & (order < starts[g + 1])
            slot = jnp.where(here, 2 * g + order - starts[g], slot)
        kinv[p] = slot
        return carry

    lax.fori_loop(0, positions, invert, 0)

    xcopies = []

    def send_chunk(h):
        for k in spiral(owners):
            zcopies[h * (owners - 1) + spiral(owners).index(k)].wait_recv()
        for k in spiral(replicas) + [0]:
            r = peer(me_dp, k, replicas)
            for c in range(CAP):
                slots[h][2 * r + c] = tiles[h][table[2 * r + c]]
        for k in spiral(replicas):
            to = peer(me_dp, k, replicas)
            xcopies.append(
                pltpu.make_async_remote_copy(
                    src_ref=slots[h].at[pl.ds(2 * to, 2)],
                    dst_ref=inc[h].at[pl.ds(2 * me_dp, 2)],
                    send_sem=xs.at[h, k],
                    recv_sem=xr.at[h, k],
                    device_id={"dp": to},
                    device_id_type=MESH,
                )
            )
            xcopies[-1].start()
        inc[h][pl.ds(2 * me_dp, 2)] = slots[h][pl.ds(2 * me_dp, 2)]

    send_chunk(0)

    for copy in ycopies:
        copy.wait_recv()
    ybuf[me_t] = part[...]
    total = ybuf[0]
    for t in range(1, tensors):
        total = total + ybuf[t]
    zbuf[me_s] = total
    zscopies = []
    for k in spiral(owners):
        to = peer(me_s, k, owners)
        zscopies.append(
            pltpu.make_async_remote_copy(
                src_ref=zbuf.at[me_s],
                dst_ref=zbuf.at[me_s],
                send_sem=zss.at[k],
                recv_sem=zsr.at[k],
                device_id={"seq": to},
                device_id_type=MESH,
            )
        )
        zscopies[-1].start()

    for h in range(1, CHUNKS):
        send_chunk(h)

    for copy in zscopies:
        copy.wait_recv()
    text_total = zbuf[0, :positions]
    for s in range(1, owners):
        text_total = text_total + zbuf[s, :positions]
    tsums[...] = text_total
    for s in range(owners):
        isums[2 * s : 2 * s + 2, :] = zbuf[s, positions : positions + 2]
    for r in range(replicas):
        for c in range(CAP):
            xsend[r, c : c + 1, :] = isums[pl.ds(table[2 * r + c], 1), :]
    xscopies = []
    for k in spiral(replicas):
        to = peer(me_dp, k, replicas)
        xscopies.append(
            pltpu.make_async_remote_copy(
                src_ref=xsend.at[to],
                dst_ref=xsums.at[me_dp],
                send_sem=xss.at[k],
                recv_sem=xsr.at[k],
                device_id={"dp": to},
                device_id_type=MESH,
            )
        )
        xscopies[-1].start()
    xsums[me_dp] = xsend[me_dp]
    for copy in xscopies:
        copy.wait_recv()

    def scale_rows(p, carry):
        slot = kinv[p]
        safe = jnp.maximum(slot, 0)
        image = xsums[safe // 2, pl.ds(lax.rem(safe, 2), 1), :]
        total = jnp.where(slot >= 0, image, tsums[pl.ds(p, 1), :])
        scale = lax.rsqrt(total / D + 1e-05)
        scales[p] = jnp.transpose(jnp.broadcast_to(scale, (TILE, TILE)))
        return carry

    lax.fori_loop(0, positions, scale_rows, 0)

    stores = []
    for h in range(CHUNKS):
        for i in range(replicas - 1):
            xcopies[h * (replicas - 1) + i].wait_recv()

        def finish(p, carry, h=h):
            slot = kinv[p]
            picked = inc[h][jnp.maximum(slot, 0)]
            here = pl.ds(h * rows, rows)
            chosen = jnp.where(slot >= 0, picked, text[p, here, :]).astype(jnp.float32)
            out[p, here, :] = (chosen * scales[p, here, :] * gain[...]).astype(jnp.bfloat16)
            return carry

        lax.fori_loop(0, positions, finish, 0)
        here = pl.ds(h * rows, rows)
        stores.append(
            pltpu.make_async_copy(out.at[:, here, :], out_hbm.at[:, here, :], osem.at[h])
        )
        stores[-1].start()

    for copy in zcopies + ycopies + zscopies + xcopies + xscopies:
        copy.wait_send()
    for copy in stores:
        copy.wait()


def local(
    vit_out, ln_gain, ln_bias, proj_weight, proj_bias, text_embed, norm_gain, tile_dest, tile_place
):
    replicas, owners, tensors = (lax.axis_size(a) for a in ("dp", "seq", "tensor"))
    local_rows = vit_out.shape[0]
    block = proj_weight.shape[2]
    positions = tile_place.shape[1]
    rows = TILE // CHUNKS
    normed_in = layer_norm(vit_out, ln_gain, ln_bias)
    weights = proj_weight.reshape(vit_out.shape[1], owners * block)
    hidden = jnp.dot(normed_in, weights, preferred_element_type=jnp.float32) + proj_bias.reshape(-1)
    projected = hidden.astype(jnp.bfloat16).reshape(2, TILE, owners, block)
    projected = jnp.transpose(projected, (2, 0, 1, 3))
    text = text_embed.reshape(positions, TILE, block)

    vmem, smem = pl.BlockSpec(memory_space=pltpu.VMEM), pl.BlockSpec(memory_space=pltpu.SMEM)
    hbm = pl.BlockSpec(memory_space=pl.ANY)
    bf16, f32, i32 = jnp.bfloat16, jnp.float32, jnp.int32
    dma = pltpu.SemaphoreType.DMA
    out = pl.pallas_call(
        functools.partial(exchange_kernel, (replicas, owners, tensors, positions)),
        out_shape=jax.ShapeDtypeStruct(text.shape, bf16),
        in_specs=[vmem, hbm, vmem, smem, smem],
        out_specs=hbm,
        scratch_shapes=[
            pltpu.VMEM(text.shape, bf16),
            pltpu.VMEM(text.shape, bf16),
            pltpu.VMEM(text.shape, f32),
            pltpu.VMEM((positions + 8, TILE), f32),
            pltpu.VMEM((tensors, positions + 8, TILE), f32),
            pltpu.VMEM((owners, positions + 8, TILE), f32),
            pltpu.VMEM((2 * owners, TILE), f32),
            pltpu.VMEM((positions, TILE), f32),
            pltpu.VMEM((replicas, 8, TILE), f32),
            pltpu.VMEM((replicas, 8, TILE), f32),
            pltpu.SMEM((CAP * replicas,), i32),
            pltpu.SMEM((positions,), i32),
            pltpu.SMEM((replicas + 1,), i32),
        ]
        + [pltpu.VMEM((2 * owners, rows, block), bf16)] * CHUNKS
        + [pltpu.VMEM((CAP * replicas, rows, block), bf16)] * CHUNKS
        + [pltpu.VMEM((CAP * replicas, rows, block), bf16)] * CHUNKS
        + [dma((CHUNKS, owners))] * 2
        + [dma((CHUNKS, replicas))] * 2
        + [dma((tensors,))] * 2
        + [dma((owners,))] * 2
        + [dma((replicas,))] * 2
        + [dma, dma((CHUNKS,))],
        compiler_params=pltpu.CompilerParams(
            collective_id=0, has_side_effects=True, vmem_limit_bytes=32 * 1024 * 1024
        ),
    )(projected, text, norm_gain.reshape(1, block), tile_dest.reshape(-1), tile_place)
    return out.reshape(text_embed.shape)


def solution(mesh):
    placed = (
        P(("dp", "seq"), None),
        P(),
        P(),
        P(None, None, "tensor"),
        P(None, "tensor"),
        P("dp", ("seq", "tensor")),
        P(("seq", "tensor")),
        P(),
        P(),
    )
    return jax.shard_map(
        local, mesh=mesh, in_specs=placed, out_specs=P("dp", ("seq", "tensor")), check_vma=False
    )
```

time: 128 us -> 74.4 us (0.58)
  Pallas kernels: 0 us -> 64.1 us
  blocking collectives: 37.2 us -> 0 us
  other arithmetic: 33.7 us -> 3.87 us
  starting transfers between devices: 24.5 us -> 0 us
  waiting for transfers between devices: 19.7 us -> 0 us
  local copies, waits for them, and re-layouts: 6.92 us -> 1.2 us
    pallas_call x0 -> x1, Pallas kernels: none -> 64.1 us  [local(): pl.pallas_call(functools.partial(exchange_kernel, (replicas, owners, tens...]
    all_to_all x1 -> x0, blocking collectives: 37.2 us -> none  [from_everyone(): return lax.all_to_all(copies, axis, split_axis=0, concat_axis=0, tiled=True)]
    all_to_all x2 -> x0, starting transfers between devices: 24.5 us -> none  [the longest x1 17.2 us: local(): lax.all_to_all(projected.reshape(local_rows, owners, column_block), 'seq'...]
    all_to_all x2 -> x0, waiting for transfers between devices: 19.7 us -> none  [the longest x1 13.7 us: local(): lax.all_to_all(projected.reshape(local_rows, owners, column_block), 'seq'...]
    select_n x5 -> x0, other arithmetic: 16.7 us -> none  [the longest x1 15.6 us: local(): jnp.where(destination == my_replica, jnp.take(place_row, jnp.minimum(rank...]
    gather x5 -> x0, other arithmetic: 4.6 us -> none  [the longest x2 4.58 us: local(): jnp.take(place_row, jnp.minimum(ranks, positions - 1))]
    convert_element_type x3 -> x0, other arithmetic: 3.82 us -> none  [the longest x1 3.74 us: local(): (assembled.astype(jnp.float32) * scale[:, None] * norm_gain).astype(jnp.b...]
    gather x5 -> x0, local copies, waits for them, and re-layouts: 3.64 us -> none  [the longest x2 1.44 us: local(): jnp.take(place_row, jnp.minimum(ranks, positions - 1))]
  transfers between devices with their start and end apart: 2 -> 0, of which waited for: 2 -> 0; matrix products, arithmetic and copies ran while one was open for 21% -> 0% of each run, Pallas kernels for 0% -> 0%
where the time goes in v1:
time: 74.4 us; the launch traced here: 74.2 us
  Pallas kernels  64.1 us (86%)
  matrix products  4.94 us (7%)
  other arithmetic  3.87 us (5%)
  local copies, waits for them, and re-layouts  1.2 us (2%)
    pallas_call x1, Pallas kernels, local(): pl.pallas_call(functools.partial(exchange_kernel, (replicas, owners, tens...  64.1 us
    dot_general x1, matrix products, local(): jnp.dot(normed_in, weights, preferred_element_type=jnp.float32)  4.94 us
    reduce_sum x1, other arithmetic, layer_norm(): spread = jnp.mean(center * center, axis=-1, keepdims=True)  2 us
    reduce_sum x1, other arithmetic, layer_norm(): center = values - jnp.mean(values, axis=-1, keepdims=True)  1.85 us

profile of v1, /device:TPU:1, one launch (start us, length us, event | category | flops | bytes accessed | tf_op | source)
XLA Modules:
  0.0 74.2 jit_solution(2299505386118250240)
XLA Ops:
  0.0 0.0 copy-start.4
  0.0 0.0 copy-start.7
  0.0 0.0 copy-start.5
  0.0 0.0 copy-start.6
  0.0 1.8 %convert_reduce_fusion = f32[256]{0:T(256)S(1)} fusion(bf16[256,3200]{1,0:T(8,128)(2,1)} %param.9), kind=kLoop, calls=%fused_computation.4 | loop fusion | flops 1638144 | bytes 1639424 | tf_op jit(solution)/shard_map/reduce_sum | solution.py:19
  1.9 2.0 %fusion.5 = f32[256]{0:T(256)S(1)} fusion(bf16[256,3200]{1,0:T(8,128)(2,1)} %param.9, f32[256]{0:T(256)S(1)} %broadcast_multiply_fusion), kind=kLoop, calls=%fused_computation.7 | loop fusion | flops 3276544 | bytes 1640448 | tf_op jit(solution)/shard_map/reduce_sum | solution.py:20
  3.9 0.0 copy-done.4
  3.9 0.0 copy-done.7
  3.9 0.0 copy-done.5
  3.9 0.0 copy-done.6
  3.9 0.0 copy-start
  3.9 0.0 copy-start.1
  4.0 0.0 copy-start.2
  4.0 0.0 copy-start.3
  4.0 4.9 %fusion.24 = bf16[32,8,8,128]{3,1,2,0:T(8,128)(2,1)S(1)} fusion(bf16[400,8,8,128]{3,2,1,0:T(8,128)(2,1)} %bitcast.28, bf16[256,3200]{1,0:T(8,128)(2,1)S(1)} %copy-done.4, f32[3200]{0:T(1024)S(1)} %copy-done.5, f32[3200]{0:T(1024)S(1)} %copy-done.6, f32[256]{0:T(256)S(1)} %add_rsqrt_fusion, f32[256]{0:T(256)S(1)} %broadcast_multiply_fusion, ...), kind=kOutput, calls=%fused_computation.17 | convolution fusion | flops 1683161088 | bytes 8748032 | tf_op jit(solution)/shard_map/dot_general | solution.py:297
  8.9 0.1 copy.12
  9.0 0.1 copy.24
  9.1 0.0 copy-done
  9.1 0.0 copy-done.1
  9.2 0.0 copy-done.2
  9.2 0.0 copy-done.3
  9.2 64.1 %shard_map.91 = bf16[32,128,128]{2,1,0:T(8,128)(2,1)S(1)} custom-call(bf16[8,2,128,128]{3,2,1,0:T(8,128)(2,1)S(1)} %bitcast.23, bf16[32,128,128]{2,1,0:T(8,128)(2,1)S(1)} %bitcast.24, f32[1,128]{1,0:T(1,128)S(1)} %bitcast.26, s32[256]{0:T(256)S(1)} %bitcast.25, s32[16,32]{1,0:T(8,128)S(1)} %copy-done.1), custom_call_target="tpu_custom_call" | custom-call | tf_op jit(solution)/shard_map/pallas_call | solution.py:306
  73.2 1.0 %copy.26 = bf16[4096,128]{1,0:T(8,128)(2,1)} copy(bf16[4096,128]{1,0:T(8,128)(2,1)S(1)} %bitcast.22) | data formatting | bytes 2097152
  (2 shorter events, 0.0 us)
Async XLA Ops:
  0.0 3.9 %copy-start.4 = (bf16[256,3200]{1,0:T(8,128)(2,1)S(1)}, bf16[256,3200]{1,0:T(8,128)(2,1)}, u32[]{:S(2)}) copy-start(bf16[256,3200]{1,0:T(8,128)(2,1)} %param.9) | copy-start | bytes 4915204
  0.0 3.9 %copy-start.7 = (f32[8,128]{1,0:T(8,128)S(1)}, f32[8,128]{1,0:T(8,128)}, u32[]{:S(2)}) copy-start(f32[8,128]{1,0:T(8,128)} %param.13) | copy-start | bytes 12292
  0.0 3.9 %copy-start.5 = (f32[3200]{0:T(1024)S(1)}, f32[3200]{0:T(1024)}, u32[]{:S(2)}) copy-start(f32[3200]{0:T(1024)} %param.11) | copy-start | bytes 38404
  0.0 3.9 %copy-start.6 = (f32[3200]{0:T(1024)S(1)}, f32[3200]{0:T(1024)}, u32[]{:S(2)}) copy-start(f32[3200]{0:T(1024)} %param.10) | copy-start | bytes 38404
  3.9 5.2 %copy-start = (bf16[4096,128]{1,0:T(8,128)(2,1)S(1)}, bf16[4096,128]{1,0:T(8,128)(2,1)}, u32[]{:S(2)}) copy-start(bf16[4096,128]{1,0:T(8,128)(2,1)} %param.14) | copy-start | bytes 3145732
  3.9 5.2 %copy-start.1 = (s32[16,32]{1,0:T(8,128)S(1)}, s32[16,32]{1,0:T(8,128)}, u32[]{:S(2)}) copy-start(s32[16,32]{1,0:T(8,128)} %place.1) | copy-start | bytes 6148
  4.0 5.2 %copy-start.2 = (s32[256,1]{0,1:T(1,128)S(1)}, s32[256,1]{0,1:T(1,128)}, u32[]{:S(2)}) copy-start(s32[256,1]{0,1:T(1,128)} %param.16) | copy-start | bytes 3076
  4.0 5.2 %copy-start.3 = (f32[128]{0:T(128)S(1)}, f32[128]{0:T(128)}, u32[]{:S(2)}) copy-start(f32[128]{0:T(128)} %param.15) | copy-start | bytes 1540

commit v2 on v1

v2 whole, which is shorter than its diff:
```python
import functools

import jax
import jax.numpy as jnp
from jax import lax
from jax.experimental import pallas as pl
from jax.experimental.pallas import tpu as pltpu
from jax.sharding import PartitionSpec as P

D = 8192
TILE = 128
CAP = 2
SPANS = (16, 16, 32, 32, 32)
CHUNKS = len(SPANS)
DEPTH = 640
LIMIT = 56
PASSES = ((0,), (1,), (2,), (3, 4))
EARLY = 3
UNROLL = 4
MESH = pl.DeviceIdType.MESH


def spiral(n):
    order = [n // 2]
    for d in range(n // 2 - 1, 0, -1):
        order += [d, n - d]
    return order


def wait_for(ref, sem):
    pltpu.make_async_copy(ref, ref, sem).wait()


def lane_sums(squares):
    ones = jnp.ones((8, squares.shape[1]), jnp.bfloat16)
    dims = (((1,), (1,)), ((), ()))
    high = squares.astype(jnp.bfloat16)
    low = (squares - high.astype(jnp.float32)).astype(jnp.bfloat16)
    return lax.dot_general(
        ones, high, dims, preferred_element_type=jnp.float32
    ) + lax.dot_general(ones, low, dims, preferred_element_type=jnp.float32)


def exchange_kernel(
    sizes,
    vit_hbm,
    weight_hbm,
    ln_gain_hbm,
    ln_bias_hbm,
    bias_hbm,
    text_hbm,
    gain_hbm,
    dest_hbm,
    place_hbm,
    out_hbm,
    out,
    ln_gain,
    ln_bias,
    bias,
    gain,
    dest,
    place,
    lgain,
    lbias,
    wraw,
    wwide,
    wflat,
    xn,
    acc,
    squares,
    text,
    scales,
    part,
    ybuf,
    zbuf,
    isums,
    tsums,
    xsend,
    xsums,
    table,
    kinv,
    starts,
    *rest,
):
    replicas, owners, tensors, positions = sizes
    group_tiles = 2 * owners
    proj, tiles, slots, inc, vit = (rest[i * CHUNKS : (i + 1) * CHUNKS] for i in range(5))
    zs, zr, xs, xr, ys, yr, zss, zsr, xss, xsr, tss, tsr, tsem, vsem, wsem, psem, osem = rest[5 * CHUNKS :]
    width, block = vit_hbm.shape[2], gain.shape[1]
    steps = width // DEPTH
    me_dp, me_s, me_t = lax.axis_index("dp"), lax.axis_index("seq"), lax.axis_index("tensor")

    def peer(me, k, n):
        return lax.rem(me + k, n)

    small = []
    for i, (source, target) in enumerate(
        (
            (ln_gain_hbm, ln_gain),
            (ln_bias_hbm, ln_bias),
            (bias_hbm, bias),
            (gain_hbm, gain),
            (dest_hbm, dest),
            (place_hbm, place),
        )
    ):
        small.append(pltpu.make_async_copy(source, target, psem.at[i]))
        small[-1].start()
    base = [sum(SPANS[:h]) for h in range(CHUNKS)]
    load_vit = []
    for h in range(CHUNKS):
        here = pl.ds(base[h], SPANS[h])
        load_vit.append(
            pltpu.make_async_copy(vit_hbm.at[:, here, :], vit[h], vsem.at[h])
        )
    load_vit[0].start()
    load_weight = []
    for i in range(steps):
        here = pl.ds(i * DEPTH * owners, DEPTH * owners)
        load_weight.append(
            pltpu.make_async_copy(weight_hbm.at[here], wraw.at[here], wsem.at[i])
        )
        load_weight[-1].start()
    for h in range(1, CHUNKS):
        load_vit[h].start()
    load_text = pltpu.make_async_copy(text_hbm, text, tsem)
    load_text.start()
    barrier = pltpu.get_barrier_semaphore()
    axes = (("dp", me_dp, replicas), ("seq", me_s, owners), ("tensor", me_t, tensors))
    for name, me, n in axes:
        for k in spiral(n):
            pl.semaphore_signal(
                barrier, inc=1, device_id={name: peer(me, k, n)}, device_id_type=MESH
            )

    def norm_chunk(h, side, first):
        load_vit[h].wait()

        def norm(g, carry):
            for i in range(2):
                rows = pl.ds(pl.multiple_of(16 * g, 16), 16)
                values = vit[h][i, rows, :].astype(jnp.float32)
                center = values - jnp.mean(values, axis=-1, keepdims=True)
                spread = jnp.mean(center * center, axis=-1, keepdims=True)
                normed = center * lax.rsqrt(spread + 1e-06) * lgain[...] + lbias[...]
                to = pl.ds(pl.multiple_of(first + i * SPANS[h] + 16 * g, 16), 16)
                xn[side, to, :] = normed.astype(jnp.bfloat16)
            return carry

        lax.fori_loop(0, SPANS[h] // 16, norm, 0)

    def keep(h, s, hidden):
        rounded = (hidden + bias[s : s + 1, :]).astype(jnp.bfloat16)
        proj[h][s] = rounded.reshape(2, SPANS[h], block)
        values = rounded.astype(jnp.float32)
        return (values * values).reshape(2, SPANS[h], block)


    def send_owners(h):
        for k in spiral(owners):
            to = peer(me_s, k, owners)
            pltpu.make_async_remote_copy(
                src_ref=proj[h].at[to],
                dst_ref=tiles[h].at[pl.ds(2 * me_s, 2)],
                send_sem=zs,
                recv_sem=zr.at[h, k],
                device_id={"seq": to},
                device_id_type=MESH,
            ).start()
        tiles[h][pl.ds(2 * me_s, 2)] = proj[h][me_s]

    small[0].wait()
    small[1].wait()
    for i in range(width // block):
        here = slice(i * block, (i + 1) * block)
        lgain[:, here] = ln_gain[i : i + 1, :]
        lbias[:, here] = ln_bias[i : i + 1, :]

    norm_chunk(0, 0, 0)
    first_rows = 2 * SPANS[0]

    def widen(i):
        load_weight[i].wait()
        here = pl.ds(i * DEPTH * owners, DEPTH * owners)
        wwide[i % 2] = wraw[here, :].astype(jnp.float32)

    widen(0)
    for i in range(steps):
        if i + 1 < steps:
            widen(i + 1)
        parts = [
            wwide[i % 2, pl.ds(s, DEPTH, stride=owners), :].astype(jnp.bfloat16)
            for s in range(owners)
        ]
        flat = jnp.concatenate(parts, axis=1)
        wflat[i * DEPTH : (i + 1) * DEPTH, :] = flat
        step = jnp.dot(
            xn[0, :first_rows, i * DEPTH : (i + 1) * DEPTH],
            flat,
            preferred_element_type=jnp.float32,
        )
        if i == 0:
            acc[...] = step
        else:
            acc[...] += step
    small[2].wait()
    total = jnp.zeros((2, SPANS[0], block), jnp.float32)
    for s in range(owners):
        total = total + keep(0, s, acc[:, s * block : (s + 1) * block])
    squares[:, 0 : SPANS[0], :] = total
    pl.semaphore_wait(barrier, replicas + owners + tensors - 3)
    send_owners(0)

    half = owners // 2

    def project(n_pass):
        rows = 0
        for h in PASSES[n_pass]:
            norm_chunk(h, n_pass % 2, rows)
            rows += 2 * SPANS[h]
        totals = [jnp.zeros((2, SPANS[h], block), jnp.float32) for h in PASSES[n_pass]]
        for n in range(2):
            hidden = jnp.dot(
                xn[n_pass % 2, :rows, :],
                wflat[:, n * half * block : (n + 1) * half * block],
                preferred_element_type=jnp.float32,
            )
            first = 0
            for i, h in enumerate(PASSES[n_pass]):
                mine = hidden[first : first + 2 * SPANS[h]]
                first += 2 * SPANS[h]
                for s in range(half):
                    columns = mine[:, s * block : (s + 1) * block]
                    totals[i] = totals[i] + keep(h, n * half + s, columns)
        for i, h in enumerate(PASSES[n_pass]):
            squares[:, base[h] : base[h] + SPANS[h], :] = totals[i]
            send_owners(h)

    for copy in small[3:]:
        copy.wait()
    for r in range(replicas):
        first = jnp.int32(group_tiles - 1)
        last = jnp.int32(0)
        for j in range(group_tiles):
            hit = dest[me_dp * group_tiles + j] == r
            last = jnp.where(hit, j, last)
            hit_back = dest[me_dp * group_tiles + group_tiles - 1 - j] == r
            first = jnp.where(hit_back, group_tiles - 1 - j, first)
        table[2 * r] = first
        table[2 * r + 1] = last

    for n_pass in range(1, EARLY):
        project(n_pass)


    def send_chunk(h):
        for k in range(1, owners):
            wait_for(tiles[h].at[pl.ds(2 * peer(me_s, owners - k, owners), 2)], zr.at[h, k])
        for k in spiral(replicas) + [0]:
            r = peer(me_dp, k, replicas)
            for c in range(CAP):
                slots[h][2 * r + c] = tiles[h][table[2 * r + c]]
        for k in spiral(replicas):
            to = peer(me_dp, k, replicas)
            pltpu.make_async_remote_copy(
                src_ref=slots[h].at[pl.ds(2 * to, 2)],
                dst_ref=inc[h].at[pl.ds(2 * me_dp, 2)],
                send_sem=xs,
                recv_sem=xr.at[h, k],
                device_id={"dp": to},
                device_id_type=MESH,
            ).start()
        inc[h][pl.ds(2 * me_dp, 2)] = slots[h][pl.ds(2 * me_dp, 2)]

    load_text.wait()
    sub = lax.broadcasted_iota(jnp.int32, (8, TILE), 0)
    share = positions // tensors

    def sum_text(t, carry):
        values = text[pl.ds(share * t, share)].astype(jnp.float32).reshape(share * TILE, TILE)
        sums = lane_sums(values * values)
        total = jnp.zeros((8, TILE), jnp.float32)
        for i in range(share):
            total = jnp.where(sub == i, sums[:, i * TILE : (i + 1) * TILE], total)
        part[t] = total
        return carry

    lax.fori_loop(0, tensors, sum_text, 0)
    send_chunk(0)
    for n_pass in range(EARLY, len(PASSES)):
        project(n_pass)
    sums = lane_sums(squares[...].reshape(2 * TILE, TILE))
    for t in range(tensors):
        for i in range(2):
            part[t, share + i : share + i + 1, :] = sums[:1, i * TILE : (i + 1) * TILE]
    for k in spiral(tensors):
        to = peer(me_t, k, tensors)
        pltpu.make_async_remote_copy(
            src_ref=part.at[to],
            dst_ref=ybuf.at[me_t],
            send_sem=ys,
            recv_sem=yr.at[k],
            device_id={"tensor": to},
            device_id_type=MESH,
        ).start()

    send_chunk(1)

    def count(g, total):
        starts[g] = total
        for j in range(group_tiles):
            total = total + jnp.where(dest[g * group_tiles + j] == me_dp, 1, 0)
        return total

    starts[replicas] = lax.fori_loop(0, replicas, count, jnp.int32(0))

    def invert(p, carry):
        order = jnp.int32(0)
        for k in range(positions):
            order = jnp.where(place[me_dp, k] == p, k, order)
        slot = jnp.int32(-1)
        for g in range(replicas):
            here = (order >= starts[g]) & (order < starts[g + 1])
            slot = jnp.where(here, 2 * g + order - starts[g], slot)
        kinv[p] = slot
        return carry

    lax.fori_loop(0, positions, invert, 0)

    for k in range(1, tensors):
        wait_for(ybuf.at[peer(me_t, tensors - k, tensors)], yr.at[k])
    ybuf[me_t] = part[me_t]
    total = ybuf[0]
    for t in range(1, tensors):
        total = total + ybuf[t]
    zbuf[me_s] = total
    for k in spiral(owners):
        to = peer(me_s, k, owners)
        pltpu.make_async_remote_copy(
            src_ref=zbuf.at[me_s],
            dst_ref=zbuf.at[me_s],
            send_sem=zss,
            recv_sem=zsr.at[k],
            device_id={"seq": to},
            device_id_type=MESH,
        ).start()

    send_chunk(2)

    for k in range(1, owners):
        wait_for(zbuf.at[peer(me_s, owners - k, owners)], zsr.at[k])
    for s in range(owners):
        isums[2 * s : 2 * s + 2, :] = zbuf[s, share : share + 2]
    for r in range(replicas):
        for c in range(CAP):
            xsend[r, c : c + 1, :] = isums[pl.ds(table[2 * r + c], 1), :]
    for k in spiral(replicas):
        to = peer(me_dp, k, replicas)
        pltpu.make_async_remote_copy(
            src_ref=xsend.at[to],
            dst_ref=xsums.at[me_dp],
            send_sem=xss,
            recv_sem=xsr.at[k],
            device_id={"dp": to},
            device_id_type=MESH,
        ).start()
    text_total = zbuf[0]
    for s in range(1, owners):
        text_total = text_total + zbuf[s]
    tsums[me_t] = text_total
    for k in spiral(tensors):
        to = peer(me_t, k, tensors)
        pltpu.make_async_remote_copy(
            src_ref=tsums.at[me_t],
            dst_ref=tsums.at[me_t],
            send_sem=tss,
            recv_sem=tsr.at[k],
            device_id={"tensor": to},
            device_id_type=MESH,
        ).start()
    for h in range(3, CHUNKS):
        send_chunk(h)
    xsums[me_dp] = xsend[me_dp]
    for k in range(1, tensors):
        wait_for(tsums.at[peer(me_t, tensors - k, tensors)], tsr.at[k])
    for k in range(1, replicas):
        wait_for(xsums.at[peer(me_dp, replicas - k, replicas)], xsr.at[k])

    def scale_rows(q, carry):
        for i in range(UNROLL):
            p = q * UNROLL + i
            slot = kinv[p]
            safe = jnp.maximum(slot, 0)
            image = xsums[safe // 2, pl.ds(lax.rem(safe, 2), 1), :]
            total = jnp.where(slot >= 0, image, tsums[p // share, pl.ds(lax.rem(p, share), 1), :])
            scale = lax.rsqrt(total / D + 1e-05)
            scales[p] = jnp.transpose(jnp.broadcast_to(scale, (TILE, TILE)))
        return carry

    lax.fori_loop(0, positions // UNROLL, scale_rows, 0)

    stores = []
    for h in range(CHUNKS):
        for k in range(1, replicas):
            slot = CAP * peer(me_dp, replicas - k, replicas)
            wait_for(inc[h].at[pl.ds(slot, CAP)], xr.at[h, k])

        here = pl.ds(base[h], SPANS[h])

        def finish(q, carry, h=h, here=here):
            for i in range(UNROLL):
                p = q * UNROLL + i
                slot = kinv[p]
                picked = inc[h][jnp.maximum(slot, 0)]
                chosen = jnp.where(slot >= 0, picked, text[p, here, :]).astype(jnp.float32)
                out[p, here, :] = (chosen * scales[p, here, :] * gain[...]).astype(jnp.bfloat16)
            return carry

        lax.fori_loop(0, positions // UNROLL, finish, 0)
        stores.append(
            pltpu.make_async_copy(out.at[:, here, :], out_hbm.at[:, here, :], osem.at[h])
        )
        stores[-1].start()

    wait_for(text.at[pl.ds(0, 2 * (owners - 1))], zs)
    wait_for(text.at[pl.ds(0, CAP * (replicas - 1))], xs)
    wait_for(ybuf.at[pl.ds(0, tensors - 1)], ys)
    wait_for(zbuf.at[pl.ds(0, owners - 1)], zss)
    wait_for(xsums.at[pl.ds(0, replicas - 1)], xss)
    wait_for(tsums.at[pl.ds(0, tensors - 1)], tss)
    for copy in stores:
        copy.wait()


def local(
    vit_out, ln_gain, ln_bias, proj_weight, proj_bias, text_embed, norm_gain, tile_dest, tile_place
):
    replicas, owners, tensors = (lax.axis_size(a) for a in ("dp", "seq", "tensor"))
    width = vit_out.shape[1]
    block = proj_weight.shape[2]
    positions = tile_place.shape[1]
    text = text_embed.reshape(positions, TILE, block)

    hbm = pl.BlockSpec(memory_space=pltpu.HBM)
    bf16, f32, i32 = jnp.bfloat16, jnp.float32, jnp.int32
    dma = pltpu.SemaphoreType.DMA

    def chunked(shape):
        return [pltpu.VMEM((*shape, span, block), bf16) for span in SPANS]

    out = pl.pallas_call(
        functools.partial(exchange_kernel, (replicas, owners, tensors, positions)),
        out_shape=jax.ShapeDtypeStruct(text.shape, bf16),
        in_specs=[hbm] * 9,
        out_specs=hbm,
        scratch_shapes=[
            pltpu.VMEM(text.shape, bf16),
            pltpu.VMEM((width // block, block), f32),
            pltpu.VMEM((width // block, block), f32),
            pltpu.VMEM(proj_bias.shape, f32),
            pltpu.VMEM((1, block), f32),
            pltpu.SMEM((tile_dest.shape[0],), i32),
            pltpu.SMEM(tile_place.shape, i32),
            pltpu.VMEM((1, width), f32),
            pltpu.VMEM((1, width), f32),
            pltpu.VMEM((width * owners, block), bf16),
            pltpu.VMEM((2, DEPTH * owners, block), f32),
            pltpu.VMEM((width, owners * block), bf16),
            pltpu.VMEM((2, 2 * max(sum(SPANS[h] for h in p) for p in PASSES), width), bf16),
            pltpu.VMEM((2 * SPANS[0], owners * block), f32),
            pltpu.VMEM((2, TILE, block), f32),
            pltpu.VMEM(text.shape, bf16),
            pltpu.VMEM(text.shape, f32),
            pltpu.VMEM((tensors, 8, TILE), f32),
            pltpu.VMEM((tensors, 8, TILE), f32),
            pltpu.VMEM((owners, 8, TILE), f32),
            pltpu.VMEM((2 * owners, TILE), f32),
            pltpu.VMEM((tensors, 8, TILE), f32),
            pltpu.VMEM((replicas, 8, TILE), f32),
            pltpu.VMEM((replicas, 8, TILE), f32),
            pltpu.SMEM((CAP * replicas,), i32),
            pltpu.SMEM((positions,), i32),
            pltpu.SMEM((replicas + 1,), i32),
        ]
        + chunked((owners, 2))
        + chunked((2 * owners,))
        + chunked((CAP * replicas,))
        + chunked((CAP * replicas,))
        + [pltpu.VMEM((2, span, width), bf16) for span in SPANS]
        + [dma, dma((CHUNKS, owners)), dma, dma((CHUNKS, replicas))]
        + [dma, dma((tensors,)), dma, dma((owners,))]
        + [dma, dma((replicas,)), dma, dma((tensors,))]
        + [dma, dma((CHUNKS,)), dma((width // DEPTH,)), dma((6,)), dma((CHUNKS,))],
        compiler_params=pltpu.CompilerParams(
            collective_id=0, has_side_effects=True, vmem_limit_bytes=LIMIT * 1024 * 1024
        ),
    )(
        vit_out.reshape(2, TILE, width),
        proj_weight.reshape(width * owners, block),
        ln_gain.reshape(-1, block),
        ln_bias.reshape(-1, block),
        proj_bias,
        text,
        norm_gain.reshape(1, block),
        tile_dest.reshape(-1),
        tile_place,
    )
    return out.reshape(text_embed.shape)


def solution(mesh):
    placed = (
        P(("dp", "seq"), None),
        P(),
        P(),
        P(None, None, "tensor"),
        P(None, "tensor"),
        P("dp", ("seq", "tensor")),
        P(("seq", "tensor")),
        P(),
        P(),
    )
    return jax.shard_map(
        local, mesh=mesh, in_specs=placed, out_specs=P("dp", ("seq", "tensor")), check_vma=False
    )
```

time: 74.4 us -> 61.1 us (0.82)
  Pallas kernels: 64.1 us -> 58.6 us
  matrix products: 4.94 us -> 0 us
  other arithmetic: 3.87 us -> 0 us
  local copies, waits for them, and re-layouts: 1.2 us -> 2.26 us
    pallas_call x1, Pallas kernels: 64.1 us -> 58.6 us  [local(): pl.pallas_call(functools.partial(exchange_kernel, (replicas, owners, tens...]
    dot_general x1 -> x0, matrix products: 4.94 us -> none  [local(): jnp.dot(normed_in, weights, preferred_element_type=jnp.float32)]
    reduce_sum x2 -> x0, other arithmetic: 3.85 us -> none  [the longest x1 2 us: layer_norm(): spread = jnp.mean(center * center, axis=-1, keepdims=True)]
    unnamed x18 -> x1, local copies, waits for them, and re-layouts: 1.11 us -> 2.26 us
where the time goes in v2:
time: 61.1 us; the launch traced here: 60.9 us
  Pallas kernels  58.6 us (96%)
  local copies, waits for them, and re-layouts  2.26 us (4%)
    pallas_call x1, Pallas kernels, local(): pl.pallas_call(functools.partial(exchange_kernel, (replicas, owners, tens...  58.6 us
    unnamed x1, local copies, waits for them, and re-layouts  2.26 us

profile of v2, /device:TPU:1, one launch (start us, length us, event | category | flops | bytes accessed | tf_op | source)
XLA Modules:
  0.0 60.9 jit_solution(7470112626591431420)
XLA Ops:
  0.0 58.6 %shard_map.91 = bf16[32,128,128]{2,1,0:T(8,128)(2,1)} custom-call(bf16[2,128,3200]{2,1,0:T(8,128)(2,1)} %bitcast.10, bf16[25600,128]{1,0:T(8,128)(2,1)} %bitcast.8, f32[25,128]{1,0:T(8,128)} %bitcast.12, f32[25,128]{1,0:T(8,128)} %bitcast.13, f32[8,128]{1,0:T(8,128)} %bias_hbm.1, bf16[32,128,128]{2,1,0:T(8,128)(2,1)} %bitcast.11, f32[1,128]{1,0:T(1,128)} %bitcast.15, ...), custom_call_target="tpu_custom_call" | custom-call | tf_op jit(solution)/shard_map/pallas_call | solution.py:451
  58.6 2.3 %copy.11 = bf16[4096,128]{1,0:T(8,128)(2,1)} copy(bf16[4096,128]{1,0:T(8,128)(2,1)} %bitcast.9) | data formatting | bytes 2097152

commit v3 on v2

--- a/solution.py
+++ b/solution.py
@@ -105,7 +105,6 @@
         )
     ):
         small.append(pltpu.make_async_copy(source, target, psem.at[i]))
-        small[-1].start()
     base = [sum(SPANS[:h]) for h in range(CHUNKS)]
     load_vit = []
     for h in range(CHUNKS):
@@ -114,17 +113,19 @@
             pltpu.make_async_copy(vit_hbm.at[:, here, :], vit[h], vsem.at[h])
         )
     load_vit[0].start()
+    for copy in small[:3]:
+        copy.start()
     load_weight = []
     for i in range(steps):
         here = pl.ds(i * DEPTH * owners, DEPTH * owners)
         load_weight.append(
             pltpu.make_async_copy(weight_hbm.at[here], wraw.at[here], wsem.at[i])
         )
-        load_weight[-1].start()
-    for h in range(1, CHUNKS):
-        load_vit[h].start()
+    for copy in load_weight:
+        copy.start()
+    for copy in small[3:]:
+        copy.start()
     load_text = pltpu.make_async_copy(text_hbm, text, tsem)
-    load_text.start()
     barrier = pltpu.get_barrier_semaphore()
     axes = (("dp", me_dp, replicas), ("seq", me_s, owners), ("tensor", me_t, tensors))
     for name, me, n in axes:
@@ -163,7 +164,7 @@
                 src_ref=proj[h].at[to],
                 dst_ref=tiles[h].at[pl.ds(2 * me_s, 2)],
                 send_sem=zs,
-                recv_sem=zr.at[h, k],
+                recv_sem=zr.at[h],
                 device_id={"seq": to},
                 device_id_type=MESH,
             ).start()
@@ -181,6 +182,10 @@
 
     def widen(i):
         load_weight[i].wait()
+        if i == max(0, steps - 2):
+            for copy in load_vit[1:]:
+                copy.start()
+            load_text.start()
         here = pl.ds(i * DEPTH * owners, DEPTH * owners)
         wwide[i % 2] = wraw[here, :].astype(jnp.float32)
 
@@ -254,8 +259,7 @@
 
 
     def send_chunk(h):
-        for k in range(1, owners):
-            wait_for(tiles[h].at[pl.ds(2 * peer(me_s, owners - k, owners), 2)], zr.at[h, k])
+        wait_for(tiles[h].at[pl.ds(0, 2 * (owners - 1))], zr.at[h])
         for k in spiral(replicas) + [0]:
             r = peer(me_dp, k, replicas)
             for c in range(CAP):
@@ -266,7 +270,7 @@
                 src_ref=slots[h].at[pl.ds(2 * to, 2)],
                 dst_ref=inc[h].at[pl.ds(2 * me_dp, 2)],
                 send_sem=xs,
-                recv_sem=xr.at[h, k],
+                recv_sem=xr.at[h],
                 device_id={"dp": to},
                 device_id_type=MESH,
             ).start()
@@ -299,7 +303,7 @@
             src_ref=part.at[to],
             dst_ref=ybuf.at[me_t],
             send_sem=ys,
-            recv_sem=yr.at[k],
+            recv_sem=yr,
             device_id={"tensor": to},
             device_id_type=MESH,
         ).start()
@@ -327,8 +331,7 @@
 
     lax.fori_loop(0, positions, invert, 0)
 
-    for k in range(1, tensors):
-        wait_for(ybuf.at[peer(me_t, tensors - k, tensors)], yr.at[k])
+    wait_for(ybuf.at[pl.ds(0, tensors - 1)], yr)
     ybuf[me_t] = part[me_t]
     total = ybuf[0]
     for t in range(1, tensors):
@@ -340,15 +343,14 @@
             src_ref=zbuf.at[me_s],
             dst_ref=zbuf.at[me_s],
             send_sem=zss,
-            recv_sem=zsr.at[k],
+            recv_sem=zsr,
             device_id={"seq": to},
             device_id_type=MESH,
         ).start()
 
     send_chunk(2)
 
-    for k in range(1, owners):
-        wait_for(zbuf.at[peer(me_s, owners - k, owners)], zsr.at[k])
+    wait_for(zbuf.at[pl.ds(0, owners - 1)], zsr)
     for s in range(owners):
         isums[2 * s : 2 * s + 2, :] = zbuf[s, share : share + 2]
     for r in range(replicas):
@@ -360,7 +362,7 @@
             src_ref=xsend.at[to],
             dst_ref=xsums.at[me_dp],
             send_sem=xss,
-            recv_sem=xsr.at[k],
+            recv_sem=xsr,
             device_id={"dp": to},
             device_id_type=MESH,
         ).start()
@@ -374,17 +376,15 @@
             src_ref=tsums.at[me_t],
             dst_ref=tsums.at[me_t],
             send_sem=tss,
-            recv_sem=tsr.at[k],
+            recv_sem=tsr,
             device_id={"tensor": to},
             device_id_type=MESH,
         ).start()
     for h in range(3, CHUNKS):
         send_chunk(h)
     xsums[me_dp] = xsend[me_dp]
-    for k in range(1, tensors):
-        wait_for(tsums.at[peer(me_t, tensors - k, tensors)], tsr.at[k])
-    for k in range(1, replicas):
-        wait_for(xsums.at[peer(me_dp, replicas - k, replicas)], xsr.at[k])
+    wait_for(tsums.at[pl.ds(0, tensors - 1)], tsr)
+    wait_for(xsums.at[pl.ds(0, replicas - 1)], xsr)
 
     def scale_rows(q, carry):
         for i in range(UNROLL):
@@ -401,9 +401,7 @@
 
     stores = []
     for h in range(CHUNKS):
-        for k in range(1, replicas):
-            slot = CAP * peer(me_dp, replicas - k, replicas)
-            wait_for(inc[h].at[pl.ds(slot, CAP)], xr.at[h, k])
+        wait_for(inc[h].at[pl.ds(0, CAP * (replicas - 1))], xr.at[h])
 
         here = pl.ds(base[h], SPANS[h])
 
@@ -430,6 +428,22 @@
     wait_for(tsums.at[pl.ds(0, tensors - 1)], tss)
     for copy in stores:
         copy.wait()
+
+
+def copy_kernel(source, target, held, in_sem, out_sem):
+    parts = in_sem.shape[0]
+    rows = held.shape[0] // parts
+    loads, stores = [], []
+    for i in range(parts):
+        here = pl.ds(i * rows, rows)
+        loads.append(pltpu.make_async_copy(source.at[here], held.at[here], in_sem.at[i]))
+        stores.append(pltpu.make_async_copy(held.at[here], target.at[here], out_sem.at[i]))
+        loads[-1].start()
+    for load, store in zip(loads, stores):
+        load.wait()
+        store.start()
+    for store in stores:
+        store.wait()
 
 
 def local(
@@ -487,9 +501,8 @@
         + chunked((CAP * replicas,))
         + chunked((CAP * replicas,))
         + [pltpu.VMEM((2, span, width), bf16) for span in SPANS]
-        + [dma, dma((CHUNKS, owners)), dma, dma((CHUNKS, replicas))]
-        + [dma, dma((tensors,)), dma, dma((owners,))]
-        + [dma, dma((replicas,)), dma, dma((tensors,))]
+        + [dma, dma((CHUNKS,))] * 2
+        + [dma] * 8
         + [dma, dma((CHUNKS,)), dma((width // DEPTH,)), dma((6,)), dma((CHUNKS,))],
         compiler_params=pltpu.CompilerParams(
             collective_id=0, has_side_effects=True, vmem_limit_bytes=LIMIT * 1024 * 1024
@@ -505,7 +518,14 @@
         tile_dest.reshape(-1),
         tile_place,
     )
-    return out.reshape(text_embed.shape)
+    return pl.pallas_call(
+        copy_kernel,
+        out_shape=jax.ShapeDtypeStruct(text.shape, bf16),
+        in_specs=[hbm],
+        out_specs=hbm,
+        scratch_shapes=[pltpu.VMEM(text.shape, bf16), dma((4,)), dma((4,))],
+        compiler_params=pltpu.CompilerParams(vmem_limit_bytes=60 * 1024 * 1024),
+    )(out).reshape(text_embed.shape)
 
 
 def solution(mesh):

time: 61.1 us -> 60.8 us (level)
  local copies, waits for them, and re-layouts: 2.26 us -> 0 us
  Pallas kernels: 58.6 us -> 60.6 us
    unnamed x1 -> x0, local copies, waits for them, and re-layouts: 2.26 us -> none
    pallas_call x0 -> x1, Pallas kernels: none -> 1.98 us  [local(): pl.pallas_call(copy_kernel, out_shape=jax.ShapeDtypeStruct(text.shape, bf...]
where the time goes in v3:
time: 60.8 us; the launch traced here: 60.7 us
  Pallas kernels  60.6 us (100%)
    pallas_call x1, Pallas kernels, local(): pl.pallas_call(functools.partial(exchange_kernel, (replicas, owners, tens...  58.7 us
    pallas_call x1, Pallas kernels, local(): pl.pallas_call(copy_kernel, out_shape=jax.ShapeDtypeStruct(text.shape, bf...  1.98 us

profile of v3, /device:TPU:1, one launch (start us, length us, event | category | flops | bytes accessed | tf_op | source)
XLA Modules:
  0.0 60.7 jit_solution(15600294800494336737)
XLA Ops:
  0.0 58.7 %shard_map.91.source = bf16[32,128,128]{2,1,0:T(8,128)(2,1)} custom-call(bf16[2,128,3200]{2,1,0:T(8,128)(2,1)} %bitcast.9, bf16[25600,128]{1,0:T(8,128)(2,1)} %bitcast.8, f32[25,128]{1,0:T(8,128)} %bitcast.11, f32[25,128]{1,0:T(8,128)} %bitcast.12, f32[8,128]{1,0:T(8,128)} %bias_hbm.1, bf16[32,128,128]{2,1,0:T(8,128)(2,1)} %bitcast.10, f32[1,128]{1,0:T(1,128)} %bitcast.14, ...), custom_call_target="tpu_custom_call" | custom-call | tf_op jit(solution)/shard_map/pallas_call | solution.py:465
  58.7 2.0 %shard_map.92 = bf16[32,128,128]{2,1,0:T(8,128)(2,1)} custom-call(bf16[32,128,128]{2,1,0:T(8,128)(2,1)} %shard_map.91.source), custom_call_target="tpu_custom_call" | custom-call | tf_op jit(solution)/shard_map/pallas_call | solution.py:521

commit v4 on v3

--- a/solution.py
+++ b/solution.py
@@ -105,6 +105,7 @@
         )
     ):
         small.append(pltpu.make_async_copy(source, target, psem.at[i]))
+        small[-1].start()
     base = [sum(SPANS[:h]) for h in range(CHUNKS)]
     load_vit = []
     for h in range(CHUNKS):
@@ -113,8 +114,6 @@
             pltpu.make_async_copy(vit_hbm.at[:, here, :], vit[h], vsem.at[h])
         )
     load_vit[0].start()
-    for copy in small[:3]:
-        copy.start()
     load_weight = []
     for i in range(steps):
         here = pl.ds(i * DEPTH * owners, DEPTH * owners)
@@ -123,9 +122,10 @@
         )
     for copy in load_weight:
         copy.start()
-    for copy in small[3:]:
+    for copy in load_vit[1:]:
         copy.start()
     load_text = pltpu.make_async_copy(text_hbm, text, tsem)
+    load_text.start()
     barrier = pltpu.get_barrier_semaphore()
     axes = (("dp", me_dp, replicas), ("seq", me_s, owners), ("tensor", me_t, tensors))
     for name, me, n in axes:
@@ -182,10 +182,6 @@
 
     def widen(i):
         load_weight[i].wait()
-        if i == max(0, steps - 2):
-            for copy in load_vit[1:]:
-                copy.start()
-            load_text.start()
         here = pl.ds(i * DEPTH * owners, DEPTH * owners)
         wwide[i % 2] = wraw[here, :].astype(jnp.float32)
 

time: 60.8 us -> 59.4 us (0.977)
  Pallas kernels: 60.6 us -> 59.2 us
    pallas_call x1, Pallas kernels: 58.7 us -> 57.2 us  [local(): pl.pallas_call(functools.partial(exchange_kernel, (replicas, owners, tens...]
where the time goes in v4:
time: 59.4 us; the launch traced here: 59.2 us
  Pallas kernels  59.2 us (100%)
    pallas_call x1, Pallas kernels, local(): pl.pallas_call(functools.partial(exchange_kernel, (replicas, owners, tens...  57.2 us
    pallas_call x1, Pallas kernels, local(): pl.pallas_call(copy_kernel, out_shape=jax.ShapeDtypeStruct(text.shape, bf...  1.98 us

profile of v4, /device:TPU:1, one launch (start us, length us, event | category | flops | bytes accessed | tf_op | source)
XLA Modules:
  0.0 59.2 jit_solution(11061344919350970781)
XLA Ops:
  0.0 57.2 %shard_map.91.source = bf16[32,128,128]{2,1,0:T(8,128)(2,1)} custom-call(bf16[2,128,3200]{2,1,0:T(8,128)(2,1)} %bitcast.9, bf16[25600,128]{1,0:T(8,128)(2,1)} %bitcast.8, f32[25,128]{1,0:T(8,128)} %bitcast.11, f32[25,128]{1,0:T(8,128)} %bitcast.12, f32[8,128]{1,0:T(8,128)} %bias_hbm.1, bf16[32,128,128]{2,1,0:T(8,128)(2,1)} %bitcast.10, f32[1,128]{1,0:T(1,128)} %bitcast.14, ...), custom_call_target="tpu_custom_call" | custom-call | tf_op jit(solution)/shard_map/pallas_call | solution.py:461
  57.2 2.0 %shard_map.92 = bf16[32,128,128]{2,1,0:T(8,128)(2,1)} custom-call(bf16[32,128,128]{2,1,0:T(8,128)(2,1)} %shard_map.91.source), custom_call_target="tpu_custom_call" | custom-call | tf_op jit(solution)/shard_map/pallas_call | solution.py:517

commit v5 on v4

--- a/solution.py
+++ b/solution.py
@@ -12,7 +12,7 @@
 CAP = 2
 SPANS = (16, 16, 32, 32, 32)
 CHUNKS = len(SPANS)
-DEPTH = 640
+DEPTH = 800
 LIMIT = 56
 PASSES = ((0,), (1,), (2,), (3, 4))
 EARLY = 3

time: 59.4 us -> 59.7 us (level)
  no operation moved by 1% of the time
where the time goes in v5:
time: 59.7 us; the launch traced here: 59.5 us
  Pallas kernels  59.5 us (100%)
    pallas_call x1, Pallas kernels, local(): pl.pallas_call(functools.partial(exchange_kernel, (replicas, owners, tens...  57.5 us
    pallas_call x1, Pallas kernels, local(): pl.pallas_call(copy_kernel, out_shape=jax.ShapeDtypeStruct(text.shape, bf...  1.98 us

profile of v5, /device:TPU:1, one launch (start us, length us, event | category | flops | bytes accessed | tf_op | source)
XLA Modules:
  0.0 59.5 jit_solution(8296605299314920136)
XLA Ops:
  0.0 57.5 %shard_map.91.source = bf16[32,128,128]{2,1,0:T(8,128)(2,1)} custom-call(bf16[2,128,3200]{2,1,0:T(8,128)(2,1)} %bitcast.9, bf16[25600,128]{1,0:T(8,128)(2,1)} %bitcast.8, f32[25,128]{1,0:T(8,128)} %bitcast.11, f32[25,128]{1,0:T(8,128)} %bitcast.12, f32[8,128]{1,0:T(8,128)} %bias_hbm.1, bf16[32,128,128]{2,1,0:T(8,128)(2,1)} %bitcast.10, f32[1,128]{1,0:T(1,128)} %bitcast.14, ...), custom_call_target="tpu_custom_call" | custom-call | tf_op jit(solution)/shard_map/pallas_call | solution.py:461
  57.5 2.0 %shard_map.92 = bf16[32,128,128]{2,1,0:T(8,128)(2,1)} custom-call(bf16[32,128,128]{2,1,0:T(8,128)(2,1)} %shard_map.91.source), custom_call_target="tpu_custom_call" | custom-call | tf_op jit(solution)/shard_map/pallas_call | solution.py:517
